TPU v7x, 32 devices: a whole 2x2x4 slice. The times are simulated.
32 devices in a mesh: member: 2 (over y), pts: 4 (over x, core), sub: 4 (over z).
Axes of the slice: x: 2, y: 2, z: 4, core: 2. Of those that a mesh axis runs over, the one named last changes fastest.
Arguments:
- spectrum: bfloat16 [1800, 32, 512], P(None, ('member', 'pts'), 'sub'), parts along dimension 1, may hold values from 0.049804688 to 2
- interaction: bfloat16 [1800, 1800], replicated, may hold values from -0.125 to 0.125
- speeds: float32 [1800], replicated, may hold values from 0.2 to 0.7
- mask: int32 [16, 512], P('pts', 'sub'), may hold values from 0 to 1, as said below
Outputs:
- evolved: bfloat16 [1800, 32, 512], P(None, ('member', 'pts'), 'sub'), parts along dimension 1
There are 2 independent parts, one for each index of `member`. A program takes and returns all parts, laid end to end along the dimension named above; an argument that names none is the same for every part. Nothing has to cross between parts.
Inputs may be any that keep to these rules, and one draw needn't show every extreme that they name: `mask`: 1 marks sea, 0 land; the share of sea differs from grid row to grid row.
All inputs are finite; a program needn't handle non-finite values.
Results may differ from a plain program's by a relative error of at most 0.0075.
Values may be sent and summed in bfloat16 or wider, within the bound.
A program may use at most 128 MiB of HBM per device.

v0:
```python
import math

import jax
import jax.numpy as jnp
from jax import lax
from jax.sharding import PartitionSpec as P

ND = 36
PROP = 2


coupling = 0.5


def extended(block, sides, width):
    for axis, dim in sides:
        count = lax.axis_size(axis)
        forward = [(i, i + 1) for i in range(count - 1)]
        backward = [(target, source) for source, target in forward]
        low = lax.ppermute(
            lax.slice_in_dim(block, block.shape[dim] - width, None, axis=dim), axis, forward
        )
        high = lax.ppermute(lax.slice_in_dim(block, 0, width, axis=dim), axis, backward)
        block = jnp.concatenate([low, block, high], axis=dim)
    return block


def courants(speeds_padded, count):
    index = jnp.arange(count, dtype=jnp.int32)
    angle = (index % ND).astype(jnp.float32) * jnp.float32(2.0 * math.pi / ND)
    return (
        (speeds_padded * jnp.cos(angle)).reshape(count, 1, 1),
        (speeds_padded * jnp.sin(angle)).reshape(count, 1, 1),
    )


def advance(field, cross, along, sea, neighbours):
    cross_up = jnp.maximum(cross, 0.0)
    cross_down = jnp.minimum(cross, 0.0)
    along_up = jnp.maximum(along, 0.0)
    along_down = jnp.minimum(along, 0.0)
    for substep in range(PROP):
        back_x, next_x, back_y, next_y = neighbours(field)
        field = (
            field
            - cross_up * (field - back_x)
            - cross_down * (next_x - field)
            - along_up * (field - back_y)
            - along_down * (next_y - field)
        ) * sea
    return field


def near_points(field):
    ext = extended(field, (("pts", 1), ("sub", 2)), 1)
    return (ext[:, :-2, 1:-1], ext[:, 2:, 1:-1], ext[:, 1:-1, :-2], ext[:, 1:-1, 2:])


def shards(spectrum, interaction, speeds, mask):
    comp_count, rows_x, cols_y = spectrum.shape
    flat = spectrum.reshape(comp_count, rows_x * cols_y)
    coupled = jnp.dot(interaction, flat, preferred_element_type=jnp.float32)
    wide = flat.astype(jnp.float32)
    sea_flat = mask.astype(jnp.float32).reshape(1, rows_x * cols_y)
    grown = (
        ((wide + coupling * wide * coupled) * sea_flat)
        .astype(jnp.bfloat16)
        .reshape(comp_count, rows_x, cols_y)
    )
    cross, along = courants(speeds, comp_count)
    field = advance(
        grown.astype(jnp.float32), cross, along, mask.astype(jnp.float32)[None], near_points
    )
    return field.astype(jnp.bfloat16)


def solution(mesh):
    placed = (P(None, ("member", "pts"), "sub"), P(), P(), P("pts", "sub"))
    return jax.shard_map(
        shards,
        mesh=mesh,
        in_specs=placed,
        out_specs=P(None, ("member", "pts"), "sub"),
        check_vma=False,
    )
```

profile of v0, /device:TPU:1, one launch (start us, length us, event | category | flops | bytes accessed | tf_op | source)
XLA Modules:
  0.0 130.5 jit_solution(7692859904708294054)
XLA Ops:
  0.0 0.7 fusion.41
  0.7 8.5 %fusion.26 = f32[1800,512]{1,0:T(8,128)S(1)} fusion(bf16[1800,1800]{1,0:T(8,128)(2,1)} %param.5, bf16[225,8,4,128]{3,2,1,0:T(4,128)(2,1)} %bitcast.15, f32[512]{0:T(512)S(1)} %get-tuple-element.20), kind=kOutput, calls=%fused_computation.46 | convolution fusion | flops 3324211200 | bytes 12011648 | tf_op jit(solution)/shard_map/dot_general | solution.py:62
  9.4 1.6 %copy-done.3 = f32[1800,512]{1,0:T(8,128)} copy-done((f32[1800,512]{1,0:T(8,128)}, f32[1800,512]{1,0:T(8,128)S(1)}, u32[]{:S(2)}) %copy-start.3) | copy-done | bytes 3686424
  11.0 1.9 %copy-done.2 = f32[1800,4,128]{2,0,1:T(8,128)} copy-done((f32[1800,4,128]{2,0,1:T(8,128)}, f32[1800,4,128]{2,0,1:T(8,128)S(1)}, u32[]{:S(2)}) %copy-start.2) | copy-done | bytes 3686424
  13.0 1.9 %collective-permute-start.1 = (f32[1800,1,128]{2,0,1:T(8,128)S(1)}, f32[1800,1,128]{2,0,1:T(8,128)S(1)}, u32[]{:S(2)}, u32[]{:S(2)}) collective-permute-start(f32[1800,1,128]{2,0,1:T(8,128)S(1)} %get-tuple-element.14), channel_id=1, source_target_pairs={{4,0},{8,4},{12,8},{5,1},{9,5},{13,9},{6,2},{10,6},{14,10},{7,3},{... | collective-permute-start | bytes 2764808 | tf_op jit(solution)/shard_map/ppermute | solution.py:23
  15.0 4.5 %collective-permute-start = (f32[1800,1,128]{2,0,1:T(8,128)S(1)}, f32[1800,1,128]{2,0,1:T(8,128)}, u32[]{:S(2)}, u32[]{:S(2)}) collective-permute-start(f32[1800,1,128]{2,0,1:T(8,128)S(1)} %get-tuple-element.13), channel_id=1, source_target_pairs={{0,4},{4,8},{8,12},{1,5},{5,9},{9,13},{2,6},{6,10},{10,14},{3,7},{... | collective-permute-start | bytes 2764808 | tf_op jit(solution)/shard_map/ppermute | solution.py:20
  19.5 5.3 %copy.79 = f32[1800,512]{0,1:T(8,128)} copy(f32[1800,512]{1,0:T(8,128)} %copy-done.3) | data formatting | bytes 7372800 | tf_op jit(solution)/shard_map/convert_element_type | solution.py:72
  24.8 3.8 %collective-permute-done.1 = f32[1800,1,128]{2,0,1:T(8,128)S(1)} collective-permute-done((f32[1800,1,128]{2,0,1:T(8,128)S(1)}, f32[1800,1,128]{2,0,1:T(8,128)S(1)}, u32[]{:S(2)}, u32[]{:S(2)}) %collective-permute-start.1) | collective-permute-done | bytes 921632 | tf_op jit(solution)/shard_map/ppermute | solution.py:23
  29.0 0.8 collective-permute-done
  29.8 1.5 %copy.58 = f32[1800,1,128]{0,2,1:T(8,128)S(1)} copy(f32[1800,1,128]{2,0,1:T(8,128)} %collective-permute-done) | data formatting | bytes 1843200 | tf_op jit(solution)/shard_map/ppermute | solution.py:20
  31.4 1.3 pad_maximum_fusion.19
  32.6 3.3 %collective-permute-start.2 = (f32[1800,6,1]{0,2,1:T(1,128)S(1)}, f32[1800,6,1]{0,2,1:T(1,128)S(1)}, u32[]{:S(2)}, u32[]{:S(2)}) collective-permute-start(f32[1800,6,1]{0,2,1:T(1,128)S(1)} %get-tuple-element.7), channel_id=1, source_target_pairs={{0,1},{1,2},{2,3},{4,5},{5,6},{6,7},{8,9},{9,10},{10,11},{12,13},{... | collective-permute-start | bytes 129608 | tf_op jit(solution)/shard_map/ppermute | solution.py:20
  36.0 1.3 collective-permute-start.3
  37.4 3.4 %collective-permute-done.3 = f32[1800,6,1]{0,2,1:T(1,128)S(1)} collective-permute-done((f32[1800,6,1]{0,2,1:T(1,128)S(1)}, f32[1800,6,1]{0,2,1:T(1,128)S(1)}, u32[]{:S(2)}, u32[]{:S(2)}) %collective-permute-start.3) | collective-permute-done | bytes 43232 | tf_op jit(solution)/shard_map/ppermute | solution.py:23
  40.8 4.4 %pad_maximum_fusion.4 = (f32[1800,4,128]{0,2,1:T(8,128)}, f32[1800,4,128]{0,2,1:T(8,128)}) fusion(f32[1800,6,1]{0,2,1:T(1,128)S(1)} %collective-permute-done.2, f32[1800,1,128]{0,2,1:T(8,128)S(1)} %copy.60, f32[1800,4,128]{0,2,1:T(8,128)S(1)} %bitcast.14, f32[1800,1,128]{0,2,1:T(8,128)S(1)} %copy.58, f32[1800,6,1]{0,2,1:T(1,128)S(1)} %collective-permute-done.3), kind=kLoop, calls=%fused_computation.6 | loop fusion | flops 5529600 | bytes 12988800 | tf_op jit(solution)/shard_map/concatenate | solution.py:24
  45.2 5.4 %copy.70 = f32[1800,4,128]{2,0,1:T(8,128)} copy(f32[1800,4,128]{0,2,1:T(8,128)} %get-tuple-element.5) | data formatting | bytes 7372800
  50.6 5.4 %copy.71 = f32[1800,4,128]{2,0,1:T(8,128)} copy(f32[1800,4,128]{0,2,1:T(8,128)} %get-tuple-element.6) | data formatting | bytes 7372800
  55.9 7.2 %fusion.22 = f32[1800,4,128]{2,0,1:T(8,128)S(1)} fusion(f32[1800,4,128]{2,0,1:T(8,128)} %copy-done.2, f32[1800,1,128]{2,0,1:T(8,128)S(1)} %collective-permute-done.1, f32[1800,1,128]{2,0,1:T(8,128)} %collective-permute-done, f32[1800,4,128]{2,0,1:T(8,128)} %copy.71, f32[1800,4,128]{2,0,1:T(8,128)} %copy.70, f32[4,128]{1,0:T(4,128)S(1)} %get-tuple-element.19, ...), kind=kLoop, calls=%fused_computation.41 | loop fusion | flops 13824000 | bytes 16619648 | tf_op jit(solution)/shard_map/mul | solution.py:44
  63.2 5.9 %collective-permute-start.4 = (f32[1800,1,128]{2,0,1:T(8,128)S(1)}, f32[1800,1,128]{2,0,1:T(8,128)S(1)}, u32[]{:S(2)}, u32[]{:S(2)}) collective-permute-start(f32[1800,1,128]{2,0,1:T(8,128)S(1)} %get-tuple-element.11), channel_id=1, source_target_pairs={{0,4},{4,8},{8,12},{1,5},{5,9},{9,13},{2,6},{6,10},{10,14},{3,7},{... | collective-permute-start | bytes 2764808 | tf_op jit(solution)/shard_map/ppermute | solution.py:20
  69.1 1.9 %collective-permute-start.5 = (f32[1800,1,128]{2,0,1:T(8,128)S(1)}, f32[1800,1,128]{2,0,1:T(8,128)S(1)}, u32[]{:S(2)}, u32[]{:S(2)}) collective-permute-start(f32[1800,1,128]{2,0,1:T(8,128)S(1)} %get-tuple-element.12), channel_id=1, source_target_pairs={{4,0},{8,4},{12,8},{5,1},{9,5},{13,9},{6,2},{10,6},{14,10},{7,3},{... | collective-permute-start | bytes 2764808 | tf_op jit(solution)/shard_map/ppermute | solution.py:23
  71.1 8.4 %collective-permute-done.4 = f32[1800,1,128]{2,0,1:T(8,128)S(1)} collective-permute-done((f32[1800,1,128]{2,0,1:T(8,128)S(1)}, f32[1800,1,128]{2,0,1:T(8,128)S(1)}, u32[]{:S(2)}, u32[]{:S(2)}) %collective-permute-start.4) | collective-permute-done | bytes 921632 | tf_op jit(solution)/shard_map/ppermute | solution.py:20
  79.5 4.4 %collective-permute-done.5 = f32[1800,1,128]{2,0,1:T(8,128)S(1)} collective-permute-done((f32[1800,1,128]{2,0,1:T(8,128)S(1)}, f32[1800,1,128]{2,0,1:T(8,128)S(1)}, u32[]{:S(2)}, u32[]{:S(2)}) %collective-permute-start.5) | collective-permute-done | bytes 921632 | tf_op jit(solution)/shard_map/ppermute | solution.py:23
  83.9 0.4 pad_maximum_fusion
  84.3 5.9 %fusion.38 = (f32[1800,6,1]{2,0,1:T(8,128)}, f32[1800,6,1]{2,0,1:T(8,128)}) fusion(f32[1800,6,128]{2,0,1:T(8,128)S(1)} %pad_maximum_fusion), kind=kLoop, calls=%fused_computation.66 | loop fusion | bytes 172800 | tf_op jit(solution)/shard_map/slice | solution.py:21
  90.2 4.5 %copy.65 = f32[1800,6,1]{0,1,2:T(8,128)S(1)} copy(f32[1800,6,1]{2,0,1:T(8,128)} %get-tuple-element.9) | data formatting | bytes 86400 | tf_op jit(solution)/shard_map/slice | solution.py:21
  94.7 3.2 %collective-permute-start.6 = (f32[1800,6,1]{0,1,2:T(8,128)S(1)}, f32[1800,6,1]{0,1,2:T(8,128)S(1)}, u32[]{:S(2)}, u32[]{:S(2)}) collective-permute-start(f32[1800,6,1]{0,1,2:T(8,128)S(1)} %copy.65), channel_id=1, source_target_pairs={{0,1},{1,2},{2,3},{4,5},{5,6},{6,7},{8,9},{9,10},{10,11},{12,13},{... | collective-permute-start | bytes 129608 | tf_op jit(solution)/shard_map/ppermute | solution.py:20
  97.9 4.5 %copy.67 = f32[1800,6,1]{0,1,2:T(8,128)S(1)} copy(f32[1800,6,1]{2,0,1:T(8,128)} %get-tuple-element.10) | data formatting | bytes 86400 | tf_op jit(solution)/shard_map/slice | solution.py:23
  102.4 1.5 %collective-permute-start.7 = (f32[1800,6,1]{0,1,2:T(8,128)S(1)}, f32[1800,6,1]{0,1,2:T(8,128)S(1)}, u32[]{:S(2)}, u32[]{:S(2)}) collective-permute-start(f32[1800,6,1]{0,1,2:T(8,128)S(1)} %copy.67), channel_id=1, source_target_pairs={{1,0},{2,1},{3,2},{5,4},{6,5},{7,6},{9,8},{10,9},{11,10},{13,12},{... | collective-permute-start | bytes 129608 | tf_op jit(solution)/shard_map/ppermute | solution.py:23
  103.9 3.7 %copy.66 = f32[1800,6,1]{2,0,1:T(8,128)} copy(f32[1800,6,1]{0,1,2:T(8,128)S(1)} %collective-permute-done.6) | data formatting | bytes 86400 | tf_op jit(solution)/shard_map/ppermute | solution.py:20
  107.7 3.7 %copy.68 = f32[1800,6,1]{2,0,1:T(8,128)} copy(f32[1800,6,1]{0,1,2:T(8,128)S(1)} %collective-permute-done.7) | data formatting | bytes 86400 | tf_op jit(solution)/shard_map/ppermute | solution.py:23
  111.4 11.4 %fusion.7 = bf16[1800,4,128]{2,0,1:T(8,128)(2,1)S(1)} fusion(f32[1800,4,128]{2,0,1:T(8,128)} %copy-done, f32[1800,6,1]{2,0,1:T(8,128)} %copy.68, f32[1800,1,128]{2,0,1:T(8,128)S(1)} %collective-permute-done.5, f32[1800,1,128]{2,0,1:T(8,128)S(1)} %collective-permute-done.4, f32[1800,6,1]{2,0,1:T(8,128)} %copy.66, f32[4,128]{1,0:T(4,128)S(1)} %get-tuple-element.19, ...), kind=kLoop, calls=%fused_computation.18 | loop fusion | flops 20275200 | bytes 7490048 | tf_op jit(solution)/shard_map/convert_element_type | solution.py:74
  122.9 7.6 %copy.69 = bf16[1800,4,128]{2,1,0:T(4,128)(2,1)} copy(bf16[1800,4,128]{2,0,1:T(8,128)(2,1)S(1)} %fusion.7) | data formatting | bytes 3686400 | tf_op jit(solution)/shard_map/convert_element_type | solution.py:74
  (16 shorter events, 0.9 us)
Async XLA Ops:
  9.2 1.8 %copy-start.3 = (f32[1800,512]{1,0:T(8,128)}, f32[1800,512]{1,0:T(8,128)S(1)}, u32[]{:S(2)}) copy-start(f32[1800,512]{1,0:T(8,128)S(1)} %fusion.26) | copy-start | bytes 11059204
  11.0 1.9 %copy-start.2 = (f32[1800,4,128]{2,0,1:T(8,128)}, f32[1800,4,128]{2,0,1:T(8,128)S(1)}, u32[]{:S(2)}) copy-start(f32[1800,4,128]{2,0,1:T(8,128)S(1)} %copy_bitcast_fusion) | copy-start | bytes 11059204
  13.0 15.6 %collective-permute-start.1 = (f32[1800,1,128]{2,0,1:T(8,128)S(1)}, f32[1800,1,128]{2,0,1:T(8,128)S(1)}, u32[]{:S(2)}, u32[]{:S(2)}) collective-permute-start(f32[1800,1,128]{2,0,1:T(8,128)S(1)} %get-tuple-element.14), channel_id=1, source_target_pairs={{4,0},{8,4},{12,8},{5,1},{9,5},{13,9},{6,2},{10,6},{14,10},{7,3},{... | collective-permute-start | bytes 2764808 | tf_op jit(solution)/shard_map/ppermute | solution.py:23
  15.0 14.9 %collective-permute-start = (f32[1800,1,128]{2,0,1:T(8,128)S(1)}, f32[1800,1,128]{2,0,1:T(8,128)}, u32[]{:S(2)}, u32[]{:S(2)}) collective-permute-start(f32[1800,1,128]{2,0,1:T(8,128)S(1)} %get-tuple-element.13), channel_id=1, source_target_pairs={{0,4},{4,8},{8,12},{1,5},{5,9},{9,13},{2,6},{6,10},{10,14},{3,7},{... | collective-permute-start | bytes 2764808 | tf_op jit(solution)/shard_map/ppermute | solution.py:20
  29.0 8.3 %copy-start.4 = (f32[1800]{0:T(1024)S(1)}, f32[1800]{0:T(1024)}, u32[]{:S(2)}) copy-start(f32[1800]{0:T(1024)} %param.6) | copy-start | bytes 21604
  31.3 9.4 %copy-start.1 = (f32[1800,512]{0,1:T(8,128)S(1)}, f32[1800,512]{0,1:T(8,128)}, u32[]{:S(2)}) copy-start(f32[1800,512]{0,1:T(8,128)} %copy.79) | copy-start | bytes 11059204
  32.6 4.7 %collective-permute-start.2 = (f32[1800,6,1]{0,2,1:T(1,128)S(1)}, f32[1800,6,1]{0,2,1:T(1,128)S(1)}, u32[]{:S(2)}, u32[]{:S(2)}) collective-permute-start(f32[1800,6,1]{0,2,1:T(1,128)S(1)} %get-tuple-element.7), channel_id=1, source_target_pairs={{0,1},{1,2},{2,3},{4,5},{5,6},{6,7},{8,9},{9,10},{10,11},{12,13},{... | collective-permute-start | bytes 129608 | tf_op jit(solution)/shard_map/ppermute | solution.py:20
  36.0 4.8 %collective-permute-start.3 = (f32[1800,6,1]{0,2,1:T(1,128)S(1)}, f32[1800,6,1]{0,2,1:T(1,128)S(1)}, u32[]{:S(2)}, u32[]{:S(2)}) collective-permute-start(f32[1800,6,1]{0,2,1:T(1,128)S(1)} %get-tuple-element.8), channel_id=1, source_target_pairs={{1,0},{2,1},{3,2},{5,4},{6,5},{7,6},{9,8},{10,9},{11,10},{13,12},{... | collective-permute-start | bytes 129608 | tf_op jit(solution)/shard_map/ppermute | solution.py:23
  63.1 20.8 %copy-start = (f32[1800,4,128]{2,0,1:T(8,128)}, f32[1800,4,128]{2,0,1:T(8,128)S(1)}, u32[]{:S(2)}) copy-start(f32[1800,4,128]{2,0,1:T(8,128)S(1)} %fusion.22) | copy-start | bytes 11059204
  63.2 16.3 %collective-permute-start.4 = (f32[1800,1,128]{2,0,1:T(8,128)S(1)}, f32[1800,1,128]{2,0,1:T(8,128)S(1)}, u32[]{:S(2)}, u32[]{:S(2)}) collective-permute-start(f32[1800,1,128]{2,0,1:T(8,128)S(1)} %get-tuple-element.11), channel_id=1, source_target_pairs={{0,4},{4,8},{8,12},{1,5},{5,9},{9,13},{2,6},{6,10},{10,14},{3,7},{... | collective-permute-start | bytes 2764808 | tf_op jit(solution)/shard_map/ppermute | solution.py:20
  69.1 14.8 %collective-permute-start.5 = (f32[1800,1,128]{2,0,1:T(8,128)S(1)}, f32[1800,1,128]{2,0,1:T(8,128)S(1)}, u32[]{:S(2)}, u32[]{:S(2)}) collective-permute-start(f32[1800,1,128]{2,0,1:T(8,128)S(1)} %get-tuple-element.12), channel_id=1, source_target_pairs={{4,0},{8,4},{12,8},{5,1},{9,5},{13,9},{6,2},{10,6},{14,10},{7,3},{... | collective-permute-start | bytes 2764808 | tf_op jit(solution)/shard_map/ppermute | solution.py:23
  94.7 9.2 %collective-permute-start.6 = (f32[1800,6,1]{0,1,2:T(8,128)S(1)}, f32[1800,6,1]{0,1,2:T(8,128)S(1)}, u32[]{:S(2)}, u32[]{:S(2)}) collective-permute-start(f32[1800,6,1]{0,1,2:T(8,128)S(1)} %copy.65), channel_id=1, source_target_pairs={{0,1},{1,2},{2,3},{4,5},{5,6},{6,7},{8,9},{9,10},{10,11},{12,13},{... | collective-permute-start | bytes 129608 | tf_op jit(solution)/shard_map/ppermute | solution.py:20
  102.4 5.2 %collective-permute-start.7 = (f32[1800,6,1]{0,1,2:T(8,128)S(1)}, f32[1800,6,1]{0,1,2:T(8,128)S(1)}, u32[]{:S(2)}, u32[]{:S(2)}) collective-permute-start(f32[1800,6,1]{0,1,2:T(8,128)S(1)} %copy.67), channel_id=1, source_target_pairs={{1,0},{2,1},{3,2},{5,4},{6,5},{7,6},{9,8},{10,9},{11,10},{13,12},{... | collective-permute-start | bytes 129608 | tf_op jit(solution)/shard_map/ppermute | solution.py:23
where the time goes:
time: 131 us; the launch traced here: 130 us
  local copies, waits for them, and re-layouts  51.9 us (40%)
  other arithmetic  25.4 us (19%)
  starting transfers between devices  23.6 us (18%)
  waiting for transfers between devices  20.9 us (16%)
  matrix products  8.5 us (6%)
    ppermute x4, starting transfers between devices, extended(): lax.ppermute(lax.slice_in_dim(block, block.shape[dim] - width, None, axis...  17 us
    unnamed x12, local copies, waits for them, and re-layouts  14.2 us
    ppermute x4, waiting for transfers between devices, extended(): lax.ppermute(lax.slice_in_dim(block, 0, width, axis=dim), axis, backward)  11.7 us
    convert_element_type x1, other arithmetic, shards(): return field.astype(jnp.bfloat16)  11.4 us
    slice x4, local copies, waits for them, and re-layouts, extended(): lax.slice_in_dim(block, block.shape[dim] - width, None, axis=dim)  10.7 us
    ppermute x4, waiting for transfers between devices, extended(): lax.ppermute(lax.slice_in_dim(block, block.shape[dim] - width, None, axis...  9.28 us
    dot_general x1, matrix products, shards(): coupled = jnp.dot(interaction, flat, preferred_element_type=jnp.float32)  8.5 us
    convert_element_type x1, local copies, waits for them, and re-layouts, shards(): return field.astype(jnp.bfloat16)  7.6 us
  transfers between devices with their start and end apart: 8, of which 5 were waited for; matrix products, arithmetic and copies ran while one was open for 11% of the time, Pallas kernels for 0%

commit v1 on v0

v1 whole, which is shorter than its diff:
```python
import functools
import math

import jax
import jax.numpy as jnp
import numpy as np
from jax import lax
from jax.experimental import pallas as pl
from jax.experimental.pallas import tpu as pltpu
from jax.sharding import PartitionSpec as P

ND = 36
PROP = 2
UNIT = 72
SUB = 8
CHUNKS = 4

coupling = 0.5


def circle():
    angle = np.arange(ND, dtype=np.int32).astype(np.float32) * np.float32(2.0 * math.pi / ND)
    angle = angle.astype(np.float64)
    return np.cos(angle).astype(np.float32), np.sin(angle).astype(np.float32)


def runs(flags):
    found, start = [], None
    for i, flag in enumerate(list(flags) + [False]):
        if flag and start is None:
            start = i
        if not flag and start is not None:
            found.append((start, i - start))
            start = None
    return found


def tables(lanes):
    cosine, sine = circle()
    d = np.arange(UNIT) % ND
    rows = [np.abs(cosine[d]), np.abs(sine[d]), cosine[d] > 0, sine[d] > 0]
    return np.stack([np.broadcast_to(r.astype(np.float32)[:, None], (UNIT, lanes)) for r in rows])


def splits(blocks):
    size = max(2, blocks // CHUNKS // 2 * 2)
    starts = list(range(0, blocks, size))
    if len(starts) > 1 and blocks - starts[-1] < size:
        starts.pop()
    return [(s, (starts[i + 1] if i + 1 < len(starts) else blocks) - s) for i, s in enumerate(starts)]


def kernel(
    rows_x, chunks, plus_runs, minus_runs, counts,
    spec_hbm, inter_hbm, speeds_ref, mask_ref, tabs_ref, out_hbm,
    specv, inter, flat, acc, field, first, column, stage, packed, halo, outv,
    xsend, xrecv, ysend, yrecv,
    load_sem, out_sem, send_sem, recv_sem,
):
    lanes = flat.shape[1] // rows_x
    blocks = field.shape[1]
    tile_count = UNIT // SUB
    px, sy = lax.axis_index("pts"), lax.axis_index("sub")
    nx, ny = counts
    partner = [{"pts": px + 1}, {"pts": px - 1}, {"sub": sy + 1}, {"sub": sy - 1}]
    sends = [px < nx - 1, px > 0, sy < ny - 1, sy > 0]
    receives = [sends[1], sends[0], sends[3], sends[2]]

    spec_copy = pltpu.make_async_copy(spec_hbm, specv, load_sem.at[len(chunks)])
    spec_copy.start()
    inter_copies = []
    for c, (start, count) in enumerate(chunks):
        part = pl.ds(start * UNIT, count * UNIT)
        copy = pltpu.make_async_copy(inter_hbm.at[part], inter.at[part], load_sem.at[c])
        copy.start()
        inter_copies.append(copy)

    barrier = pltpu.get_barrier_semaphore()
    for kind in range(4):
        @pl.when(sends[kind])
        def _():
            pl.semaphore_signal(
                barrier, inc=1, device_id=partner[kind], device_id_type=pl.DeviceIdType.MESH
            )

    def exchange(e, c, kind):
        start, count = chunks[c]
        part = pl.ds(start, count)
        if kind < 2:
            source, target = xsend.at[e, kind, part], xrecv.at[e, kind, part]
        else:
            source, target = ysend.at[e, part], yrecv.at[e, kind - 2, part]
        return pltpu.make_async_remote_copy(
            src_ref=source, dst_ref=target,
            send_sem=send_sem.at[e, c, kind], recv_sem=recv_sem.at[e, c, kind],
            device_id=partner[kind], device_id_type=pl.DeviceIdType.MESH,
        )

    def start_sends(e, c):
        for kind in range(4):
            @pl.when(sends[kind])
            def _():
                exchange(e, c, kind).start()

    def wait_receives(e, c):
        for kind in range(4):
            @pl.when(receives[kind])
            def _():
                exchange(e, c, kind).wait_recv()

    for kind in range(4):
        @pl.when(jnp.logical_not(receives[kind]))
        def _():
            for e in range(PROP):
                if kind < 2:
                    xrecv[e, kind] = jnp.zeros(xrecv.shape[2:], xrecv.dtype)
                else:
                    yrecv[e, kind - 2] = jnp.zeros(yrecv.shape[2:], yrecv.dtype)

    for i in range(speeds_ref.shape[0]):
        row = jnp.broadcast_to(speeds_ref[i : i + 1, :], (lanes, lanes))
        column[i * lanes : (i + 1) * lanes, :] = row.T

    spec_copy.wait()

    def spread(block, count):
        length = count * UNIT
        whole = specv[pl.ds(pl.multiple_of(block * (rows_x * UNIT), 16), rows_x * length), :]
        stage[0 : rows_x * length, :] = whole.astype(jnp.float32)
        for x in range(rows_x):
            values = stage[pl.ds(x, length, stride=rows_x), :]
            flat[pl.ds(pl.multiple_of(block * UNIT, 16), length), x * lanes : (x + 1) * lanes] = (
                values.astype(jnp.bfloat16)
            )
            for b in range(count):
                field[x, block + b] = values[b * UNIT : (b + 1) * UNIT]

    @pl.loop(0, blocks // 2)
    def _(i):
        spread(2 * i, 2)

    if blocks % 2:
        spread(blocks - 1, 1)

    pl.semaphore_wait(barrier, sum(s.astype(jnp.int32) for s in sends))

    lane = lax.broadcasted_iota(jnp.int32, (SUB, lanes), 1)
    sea = [
        jnp.broadcast_to(mask_ref[x : x + 1, :].astype(jnp.float32), (UNIT, lanes))
        for x in range(rows_x)
    ]

    def pack(e, block, values):
        for kind, group, x in ((0, plus_runs, rows_x - 1), (1, minus_runs, 0)):
            at = 0
            for start, length in group:
                packed[kind, at : at + length, :] = values[x][start : start + length]
                at += length
            xsend[e, kind, block] = packed[kind].astype(xsend.dtype)
        message = jnp.zeros((SUB, lanes), jnp.float32)
        for t in range(tile_count):
            for x in range(rows_x):
                j = t * rows_x + x
                turned = pltpu.roll(values[x][t * SUB : (t + 1) * SUB], 2 * j + 1, 1)
                message = jnp.where((lane >= 2 * j) & (lane < 2 * j + 2), turned, message)
        ysend[e, block] = message

    def grow(c):
        start, count = chunks[c]

        @pl.loop(0, count)
        def _(i):
            block = start + i
            values = []
            for x in range(rows_x):
                wide = field[x, block]
                coupled = acc[pl.ds(pl.multiple_of(i * UNIT, SUB), UNIT), x * lanes : (x + 1) * lanes]
                grown = (wide + coupling * wide * coupled) * sea[x]
                grown = grown.astype(jnp.bfloat16).astype(jnp.float32)
                field[x, block] = grown
                values.append(grown)
            pack(0, block, values)

    def advance(e, c, source, finish):
        start, count = chunks[c]

        @pl.loop(0, count)
        def _(i):
            block = start + i
            for kind, group in ((0, plus_runs), (1, minus_runs)):
                arrived = xrecv[e, kind, block].astype(jnp.float32)
                packed[kind] = arrived
                at = 0
                for first_row, length in group:
                    halo[first_row : first_row + length, :] = packed[kind, at : at + length, :]
                    at += length
            edges = jnp.where(lane % 2 == 0, pltpu.roll(yrecv[e, 0, block], 2, 1), yrecv[e, 1, block])
            speed = column[pl.ds(pl.multiple_of(block * UNIT, SUB), UNIT), :]
            cross, along = speed * tabs_ref[0], speed * tabs_ref[1]
            results = [[] for _ in range(rows_x)]
            for t in range(tile_count):
                part = slice(t * SUB, (t + 1) * SUB)
                up_x, up_y = tabs_ref[2, part, :] > 0.5, tabs_ref[3, part, :] > 0.5
                edge = (up_y & (lane == 0)) | (jnp.logical_not(up_y) & (lane == lanes - 1))
                tiles = [source[x, block, part, :] for x in range(rows_x)]
                for x in range(rows_x):
                    j = t * rows_x + x
                    here = tiles[x]
                    lower = tiles[x - 1] if x > 0 else halo[part, :]
                    higher = tiles[x + 1] if x < rows_x - 1 else halo[part, :]
                    near_x = jnp.where(up_x, lower, higher)
                    near_y = jnp.where(up_y, pltpu.roll(here, 1, 1), pltpu.roll(here, lanes - 1, 1))
                    near_y = jnp.where(edge, pltpu.roll(edges, lanes - (2 * j + 2), 1), near_y)
                    results[x].append(
                        (here - cross[part] * (here - near_x) - along[part] * (here - near_y))
                        * sea[x][part]
                    )
            finish(block, [jnp.concatenate(r, axis=0) for r in results])

    def keep(block, values):
        for x in range(rows_x):
            first[x, block] = values[x]
        pack(1, block, values)

    def write(block, values):
        for x in range(rows_x):
            stage[pl.ds(x, UNIT, stride=rows_x), :] = values[x]
        size = rows_x * UNIT
        outv[pl.ds(pl.multiple_of(block * size, 16), size), :] = stage[0:size, :].astype(outv.dtype)

    out_copies = []
    for step in range(len(chunks) + 2):
        if step < len(chunks):
            start, count = chunks[step]
            inter_copies[step].wait()
            acc[0 : count * UNIT, :] = jnp.dot(
                inter[start * UNIT : (start + count) * UNIT, :], flat[...],
                preferred_element_type=jnp.float32,
            )
            grow(step)
            start_sends(0, step)
        if 0 <= step - 1 < len(chunks):
            wait_receives(0, step - 1)
            advance(0, step - 1, field, keep)
            start_sends(1, step - 1)
        if 0 <= step - 2:
            c = step - 2
            wait_receives(1, c)
            advance(1, c, first, write)
            start, count = chunks[c]
            part = pl.ds(start * UNIT * rows_x, count * UNIT * rows_x)
            copy = pltpu.make_async_copy(outv.at[part], out_hbm.at[part], out_sem.at[c])
            copy.start()
            out_copies.append(copy)

    for e in range(PROP):
        for c in range(len(chunks)):
            for kind in range(4):
                @pl.when(sends[kind])
                def _():
                    exchange(e, c, kind).wait_send()
    for copy in out_copies:
        copy.wait()


def shards(mesh_counts, spectrum, interaction, speeds, mask):
    comps, rows_x, lanes = spectrum.shape
    blocks = comps // UNIT
    chunks = splits(blocks)
    most = max(count for _, count in chunks)
    cosine, sine = circle()
    plus = cosine[np.arange(UNIT) % ND] > 0
    plus_runs, minus_runs = runs(plus), runs(~plus)
    half = max(int(plus.sum()), int((~plus).sum()))
    padded = -(-comps // lanes)
    speeds_rows = jnp.pad(speeds, (0, padded * lanes - comps)).reshape(padded, lanes)
    any_space = pl.BlockSpec(memory_space=pl.ANY)
    vmem = pl.BlockSpec(memory_space=pltpu.VMEM)
    f32, bf16 = jnp.float32, jnp.bfloat16
    out = pl.pallas_call(
        functools.partial(kernel, rows_x, chunks, plus_runs, minus_runs, mesh_counts),
        out_shape=jax.ShapeDtypeStruct((comps * rows_x, lanes), bf16),
        in_specs=[any_space, any_space, vmem, vmem, vmem],
        out_specs=any_space,
        scratch_shapes=[
            pltpu.VMEM((comps * rows_x, lanes), bf16),
            pltpu.VMEM((comps, comps), bf16),
            pltpu.VMEM((comps, rows_x * lanes), bf16),
            pltpu.VMEM((most * UNIT, rows_x * lanes), f32),
            pltpu.VMEM((rows_x, blocks, UNIT, lanes), f32),
            pltpu.VMEM((rows_x, blocks, UNIT, lanes), f32),
            pltpu.VMEM((padded * lanes, lanes), f32),
            pltpu.VMEM((2 * UNIT * rows_x, lanes), f32),
            pltpu.VMEM((2, half, lanes), f32),
            pltpu.VMEM((UNIT, lanes), f32),
            pltpu.VMEM((comps * rows_x, lanes), bf16),
            pltpu.VMEM((PROP, 2, blocks, half, lanes), bf16),
            pltpu.VMEM((PROP, 2, blocks, half, lanes), bf16),
            pltpu.VMEM((PROP, blocks, SUB, lanes), f32),
            pltpu.VMEM((PROP, 2, blocks, SUB, lanes), f32),
            pltpu.SemaphoreType.DMA((len(chunks) + 1,)),
            pltpu.SemaphoreType.DMA((len(chunks),)),
            pltpu.SemaphoreType.DMA((PROP, len(chunks), 4)),
            pltpu.SemaphoreType.DMA((PROP, len(chunks), 4)),
        ],
        compiler_params=pltpu.CompilerParams(
            collective_id=0, has_side_effects=True, vmem_limit_bytes=60 * 1024 * 1024
        ),
    )(
        spectrum.reshape(comps * rows_x, lanes), interaction, speeds_rows, mask,
        jnp.asarray(tables(lanes)),
    )
    return out.reshape(comps, rows_x, lanes)


def solution(mesh):
    placed = (P(None, ("member", "pts"), "sub"), P(), P(), P("pts", "sub"))
    return jax.shard_map(
        functools.partial(shards, (mesh.shape["pts"], mesh.shape["sub"])),
        mesh=mesh,
        in_specs=placed,
        out_specs=P(None, ("member", "pts"), "sub"),
        check_vma=False,
    )
```

time: 131 us -> 35.2 us (0.27)
  local copies, waits for them, and re-layouts: 51.9 us -> 4.06 us
  Pallas kernels: 0 us -> 30.8 us
  other arithmetic: 25.4 us -> 0 us
  starting transfers between devices: 23.6 us -> 0 us
  waiting for transfers between devices: 20.9 us -> 0 us
  matrix products: 8.5 us -> 0 us
    pallas_call x0 -> x1, Pallas kernels: none -> 30.8 us  [shards(): pl.pallas_call(functools.partial(kernel, rows_x, chunks, plus_runs, minus...]
    ppermute x8 -> x0, starting transfers between devices: 23.6 us -> none  [the longest x4 17 us: extended(): lax.ppermute(lax.slice_in_dim(block, block.shape[dim] - width, None, axis...]
    ppermute x8 -> x0, waiting for transfers between devices: 20.9 us -> none  [the longest x4 11.7 us: extended(): lax.ppermute(lax.slice_in_dim(block, 0, width, axis=dim), axis, backward)]
    slice x5 -> x0, local copies, waits for them, and re-layouts: 15.2 us -> none  [the longest x4 10.7 us: extended(): lax.slice_in_dim(block, block.shape[dim] - width, None, axis=dim)]
    convert_element_type x3 -> x0, local copies, waits for them, and re-layouts: 13.2 us -> none  [the longest x1 7.6 us: shards(): return field.astype(jnp.bfloat16)]
    convert_element_type x2 -> x0, other arithmetic: 12.1 us -> none  [the longest x1 11.4 us: shards(): return field.astype(jnp.bfloat16)]
    unnamed x12 -> x1, local copies, waits for them, and re-layouts: 14.2 us -> 2.76 us
    ppermute x4 -> x0, local copies, waits for them, and re-layouts: 9.3 us -> none  [the longest x2 5.24 us: extended(): lax.ppermute(lax.slice_in_dim(block, block.shape[dim] - width, None, axis...]
  transfers between devices with their start and end apart: 8 -> 0, of which waited for: 5 -> 0; matrix products, arithmetic and copies ran while one was open for 11% -> 0% of each run, Pallas kernels for 0% -> 0%
where the time goes in v1:
time: 35.2 us; the launch traced here: 34.8 us
  Pallas kernels  30.8 us (88%)
  local copies, waits for them, and re-layouts  4.06 us (12%)
    pallas_call x1, Pallas kernels, shards(): pl.pallas_call(functools.partial(kernel, rows_x, chunks, plus_runs, minus...  30.8 us
    unnamed x1, local copies, waits for them, and re-layouts  2.76 us
    reshape x1, local copies, waits for them, and re-layouts, shards(): jnp.pad(speeds, (0, padded * lanes - comps)).reshape(padded, lanes)  1.3 us

profile of v1, /device:TPU:1, one launch (start us, length us, event | category | flops | bytes accessed | tf_op | source)
XLA Modules:
  0.0 34.8 jit_solution(4098430872721109951)
XLA Ops:
  0.0 1.3 %pad_bitcast_fusion.speeds_ref = f32[15,128]{1,0:T(8,128)} fusion(f32[1800]{0:T(1024)} %param.7), kind=kLoop, calls=%fused_computation | loop fusion | bytes 14880 | tf_op jit(solution)/shard_map/reshape | solution.py:276
  1.3 30.8 %shard_map.55 = bf16[7200,128]{1,0:T(8,128)(2,1)} custom-call(bf16[7200,128]{1,0:T(8,128)(2,1)} %bitcast.5, bf16[1800,1800]{1,0:T(8,128)(2,1)} %inter_hbm.1, f32[15,128]{1,0:T(8,128)} %pad_bitcast_fusion.speeds_ref, s32[4,128]{1,0:T(4,128)} %mask_ref.1, f32[4,72,128]{2,1,0:T(8,128)} %constant.5.clone.tabs_ref), custom_call_target="tpu_custom_call" | custom-call | tf_op jit(solution)/shard_map/pallas_call | solution.py:280
  32.1 2.8 %copy.7 = bf16[1800,4,128]{2,1,0:T(4,128)(2,1)} copy(bf16[1800,4,128]{2,1,0:T(4,128)(2,1)} %bitcast.4) | data formatting | bytes 3686400

commit v2 on v1

v2 whole, which is shorter than its diff:
```python
import functools
import math

import jax
import jax.numpy as jnp
import numpy as np
from jax import lax
from jax.experimental import pallas as pl
from jax.experimental.pallas import tpu as pltpu
from jax.sharding import PartitionSpec as P

ND = 36
PROP = 2
UNIT = 72
SUB = 8
CHUNKS = 4
SLOTS = 1

coupling = 0.5


def circle():
    angle = np.arange(ND, dtype=np.int32).astype(np.float32) * np.float32(2.0 * math.pi / ND)
    angle = angle.astype(np.float64)
    return np.cos(angle).astype(np.float32), np.sin(angle).astype(np.float32)


def runs(flags):
    found, start = [], None
    for i, flag in enumerate(list(flags) + [False]):
        if flag and start is None:
            start = i
        if not flag and start is not None:
            found.append((start, i - start))
            start = None
    return found


def tables(lanes):
    cosine, sine = circle()
    d = np.arange(UNIT) % ND
    rows = [np.abs(cosine[d]), np.abs(sine[d]), cosine[d] > 0, sine[d] > 0]
    return np.stack([np.broadcast_to(r.astype(np.float32)[:, None], (UNIT, lanes)) for r in rows])


def splits(blocks):
    size = max(2, blocks // CHUNKS // 2 * 2)
    starts = list(range(0, blocks, size))
    if len(starts) > 1 and blocks - starts[-1] < size:
        starts.pop()
    return [(s, (starts[i + 1] if i + 1 < len(starts) else blocks) - s) for i, s in enumerate(starts)]


def kernel(
    rows_x, chunks, plus_runs, minus_runs, counts,
    spec_hbm, inter_hbm, speeds_ref, mask_ref, tabs_ref, outv,
    specv, inter, flat, acc, field, first, column, stage, outs, packed, arrived, halo,
    xsend, xrecv, ysend, yrecv,
    load_sem, send_sem, recv_sem,
):
    lanes = flat.shape[1] // rows_x
    blocks = field.shape[1]
    tile_count = UNIT // SUB
    px, sy = lax.axis_index("pts"), lax.axis_index("sub")
    nx, ny = counts
    partner = [{"pts": px + 1}, {"pts": px - 1}, {"sub": sy + 1}, {"sub": sy - 1}]
    sends = [px < nx - 1, px > 0, sy < ny - 1, sy > 0]
    receives = [sends[1], sends[0], sends[3], sends[2]]

    spec_copy = pltpu.make_async_copy(spec_hbm, specv, load_sem.at[len(chunks)])
    spec_copy.start()
    inter_copies = []
    for c, (start, count) in enumerate(chunks):
        part = pl.ds(start * UNIT, count * UNIT)
        copy = pltpu.make_async_copy(inter_hbm.at[part], inter.at[part], load_sem.at[c])
        copy.start()
        inter_copies.append(copy)

    barrier = pltpu.get_barrier_semaphore()
    for kind in range(4):
        @pl.when(sends[kind])
        def _():
            pl.semaphore_signal(
                barrier, inc=1, device_id=partner[kind], device_id_type=pl.DeviceIdType.MESH
            )

    def exchange(e, c, kind):
        start, count = chunks[c]
        part = pl.ds(start, count)
        if kind < 2:
            source, target = xsend.at[e, kind, part], xrecv.at[e, kind, part]
        else:
            source, target = ysend.at[e, part], yrecv.at[e, kind - 2, part]
        return pltpu.make_async_remote_copy(
            src_ref=source, dst_ref=target,
            send_sem=send_sem.at[e, c, kind], recv_sem=recv_sem.at[e, c, kind],
            device_id=partner[kind], device_id_type=pl.DeviceIdType.MESH,
        )

    def start_sends(e, c):
        for kind in range(4):
            @pl.when(sends[kind])
            def _():
                exchange(e, c, kind).start()

    def wait_receives(e, c):
        for kind in range(4):
            @pl.when(receives[kind])
            def _():
                exchange(e, c, kind).wait_recv()

    for kind in range(4):
        @pl.when(jnp.logical_not(receives[kind]))
        def _():
            for e in range(PROP):
                if kind < 2:
                    xrecv[e, kind] = jnp.zeros(xrecv.shape[2:], xrecv.dtype)
                else:
                    yrecv[e, kind - 2] = jnp.zeros(yrecv.shape[2:], yrecv.dtype)

    comps = flat.shape[0]
    starts = list(range(0, comps - lanes + 1, lanes))
    if comps % lanes:
        starts.append(comps - lanes)
    for at in starts:
        row = jnp.broadcast_to(speeds_ref[0:1, at : at + lanes], (lanes, lanes))
        column[at : at + lanes, :] = row.T

    spec_copy.wait()

    def spread(block, count):
        length = count * UNIT
        whole = specv[pl.ds(pl.multiple_of(block * (rows_x * UNIT), 16), rows_x * length), :]
        stage[0 : rows_x * length, :] = whole.astype(jnp.float32)
        for x in range(rows_x):
            values = stage[pl.ds(x, length, stride=rows_x), :]
            flat[pl.ds(pl.multiple_of(block * UNIT, 16), length), x * lanes : (x + 1) * lanes] = (
                values.astype(jnp.bfloat16)
            )
            for b in range(count):
                field[x, block + b] = values[b * UNIT : (b + 1) * UNIT]

    @pl.loop(0, blocks // 2)
    def _(i):
        spread(2 * i, 2)

    if blocks % 2:
        spread(blocks - 1, 1)

    pl.semaphore_wait(barrier, sum(s.astype(jnp.int32) for s in sends))

    lane = lax.broadcasted_iota(jnp.int32, (SUB, lanes), 1)
    pair = lane // 2
    even = lane % 2 == 0
    sea = [
        jnp.broadcast_to(mask_ref[x : x + 1, :].astype(jnp.float32), (SUB, lanes))
        for x in range(rows_x)
    ]
    cosine, sine = (np.resize(v, UNIT).reshape(tile_count, SUB) for v in circle())

    def sides(t):
        found = []
        for values in (cosine[t], sine[t]):
            if np.all(values >= 0):
                found.append(True)
            elif np.all(values <= 0):
                found.append(False)
            else:
                found.append(None)
        return found

    def pack_x(e, block, slot, source):
        for kind, group, x in ((0, plus_runs, rows_x - 1), (1, minus_runs, 0)):
            at = 0
            for begin, length in group:
                packed[slot, kind, at : at + length, :] = source[x, block, begin : begin + length, :]
                at += length
            xsend[e, kind, block] = packed[slot, kind].astype(xsend.dtype)

    def grow_block(base, i, slot):
        block = base + i
        message = jnp.zeros((SUB, lanes), jnp.float32)
        for t in range(tile_count):
            part = slice(t * SUB, (t + 1) * SUB)
            place = pl.ds(pl.multiple_of(i * UNIT, SUB) + t * SUB, SUB)
            for x in range(rows_x):
                wide = field[x, block, part, :]
                coupled = acc[place, x * lanes : (x + 1) * lanes]
                grown = (wide + coupling * wide * coupled) * sea[x]
                grown = grown.astype(jnp.bfloat16).astype(jnp.float32)
                field[x, block, part, :] = grown
                j = t * rows_x + x
                message = jnp.where(pair == j, pltpu.roll(grown, 2 * j + 1, 1), message)
        ysend[0, block] = message
        pack_x(0, block, slot, field)

    def halos(e, block, slot):
        for kind, group in ((0, plus_runs), (1, minus_runs)):
            arrived[slot, kind] = xrecv[e, kind, block].astype(jnp.float32)
            at = 0
            for begin, length in group:
                halo[slot, begin : begin + length, :] = arrived[slot, kind, at : at + length, :]
                at += length

    def advance_block(e, block, slot):
        source = field if e == 0 else first
        results = []
        edges = jnp.where(even, pltpu.roll(yrecv[e, 0, block], 2, 1), yrecv[e, 1, block])
        message = jnp.zeros((SUB, lanes), jnp.float32)
        for t in range(tile_count):
            part = slice(t * SUB, (t + 1) * SUB)
            speed = column[pl.ds(pl.multiple_of(block * UNIT, SUB) + t * SUB, SUB), :]
            cross, along = speed * tabs_ref[0, part, :], speed * tabs_ref[1, part, :]
            side_x, side_y = sides(t)
            up_x = tabs_ref[2, part, :] > 0.5 if side_x is None else None
            if side_y is None:
                up_y = tabs_ref[3, part, :] > 0.5
                edge = jnp.where(up_y, lane, lanes - 1 - lane) == 0
            else:
                edge = lane == (0 if side_y else lanes - 1)
            tiles = [source[x, block, part, :] for x in range(rows_x)]
            outer = halo[slot, part, :]
            for x in range(rows_x):
                j = t * rows_x + x
                here = tiles[x]
                lower = tiles[x - 1] if x > 0 else outer
                higher = tiles[x + 1] if x < rows_x - 1 else outer
                if side_x is None:
                    near_x = jnp.where(up_x, lower, higher)
                else:
                    near_x = lower if side_x else higher
                if side_y is None:
                    near_y = jnp.where(up_y, pltpu.roll(here, 1, 1), pltpu.roll(here, lanes - 1, 1))
                else:
                    near_y = pltpu.roll(here, 1 if side_y else lanes - 1, 1)
                near_y = jnp.where(edge, pltpu.roll(edges, lanes - (2 * j + 2), 1), near_y)
                result = (here - cross * (here - near_x) - along * (here - near_y)) * sea[x]
                results.append(result)
                if e == 0:
                    message = jnp.where(pair == j, pltpu.roll(result, 2 * j + 1, 1), message)
        for t in range(tile_count):
            for x in range(rows_x):
                result = results[t * rows_x + x]
                if e == 0:
                    first[x, block, t * SUB : (t + 1) * SUB, :] = result
                else:
                    outs[slot, pl.ds(x + t * SUB * rows_x, SUB, stride=rows_x), :] = result
        if e == 0:
            ysend[1, block] = message
            pack_x(1, block, slot, first)
        else:
            size = rows_x * UNIT
            outv[pl.ds(pl.multiple_of(block * size, 16), size), :] = outs[slot].astype(outv.dtype)

    def several(count, body):
        @pl.loop(0, count // SLOTS)
        def _(i):
            body([i * SLOTS + u for u in range(SLOTS)])

        if count % SLOTS:
            body([count - count % SLOTS + u for u in range(count % SLOTS)])

    def multiply(c):
        start, count = chunks[c]
        inter_copies[c].wait()
        acc[0 : count * UNIT, :] = jnp.dot(
            inter[start * UNIT : (start + count) * UNIT, :], flat[...],
            preferred_element_type=jnp.float32,
        )

        def body(which):
            for slot, i in enumerate(which):
                grow_block(start, i, slot)

        several(count, body)
        start_sends(0, c)

    def advance(e, c):
        start, count = chunks[c]
        wait_receives(e, c)

        def body(which):
            for slot, i in enumerate(which):
                halos(e, start + i, slot)
            for slot, i in enumerate(which):
                advance_block(e, start + i, slot)

        several(count, body)
        if e == 0:
            start_sends(1, c)

    total = len(chunks)
    for c in range(total):
        multiply(c)
        if c >= 2:
            advance(0, c - 2)
    if total >= 2:
        advance(0, total - 2)
    for c in range(total - 3):
        advance(1, c)
    advance(0, total - 1)
    for c in range(max(total - 3, 0), total):
        advance(1, c)

    for e in range(PROP):
        for c in range(len(chunks)):
            for kind in range(4):
                @pl.when(sends[kind])
                def _():
                    exchange(e, c, kind).wait_send()


def flush(held, out_hbm, sem):
    copy = pltpu.make_async_copy(held, out_hbm, sem)
    copy.start()
    copy.wait()


def shards(mesh_counts, spectrum, interaction, speeds, mask):
    comps, rows_x, lanes = spectrum.shape
    blocks = comps // UNIT
    chunks = splits(blocks)
    most = max(count for _, count in chunks)
    cosine, sine = circle()
    plus = cosine[np.arange(UNIT) % ND] > 0
    plus_runs, minus_runs = runs(plus), runs(~plus)
    half = max(int(plus.sum()), int((~plus).sum()))
    any_space = pl.BlockSpec(memory_space=pltpu.HBM)
    vmem = pl.BlockSpec(memory_space=pltpu.VMEM)
    f32, bf16 = jnp.float32, jnp.bfloat16
    out = pl.pallas_call(
        functools.partial(kernel, rows_x, chunks, plus_runs, minus_runs, mesh_counts),
        out_shape=jax.ShapeDtypeStruct((comps * rows_x, lanes), bf16),
        in_specs=[any_space, any_space, vmem, vmem, vmem],
        out_specs=vmem,
        scratch_shapes=[
            pltpu.VMEM((comps * rows_x, lanes), bf16),
            pltpu.VMEM((comps, comps), bf16),
            pltpu.VMEM((comps, rows_x * lanes), bf16),
            pltpu.VMEM((most * UNIT, rows_x * lanes), f32),
            pltpu.VMEM((rows_x, blocks, UNIT, lanes), f32),
            pltpu.VMEM((rows_x, blocks, UNIT, lanes), f32),
            pltpu.VMEM((comps, lanes), f32),
            pltpu.VMEM((2 * UNIT * rows_x, lanes), f32),
            pltpu.VMEM((SLOTS, UNIT * rows_x, lanes), f32),
            pltpu.VMEM((SLOTS, 2, half, lanes), f32),
            pltpu.VMEM((SLOTS, 2, half, lanes), f32),
            pltpu.VMEM((SLOTS, UNIT, lanes), f32),
            pltpu.VMEM((PROP, 2, blocks, half, lanes), bf16),
            pltpu.VMEM((PROP, 2, blocks, half, lanes), bf16),
            pltpu.VMEM((PROP, blocks, SUB, lanes), f32),
            pltpu.VMEM((PROP, 2, blocks, SUB, lanes), f32),
            pltpu.SemaphoreType.DMA((len(chunks) + 1,)),
            pltpu.SemaphoreType.DMA((PROP, len(chunks), 4)),
            pltpu.SemaphoreType.DMA((PROP, len(chunks), 4)),
        ],
        compiler_params=pltpu.CompilerParams(
            collective_id=0, has_side_effects=True, vmem_limit_bytes=62 * 1024 * 1024
        ),
    )(
        spectrum.reshape(comps * rows_x, lanes), interaction, speeds.reshape(1, comps), mask,
        jnp.asarray(tables(lanes)),
    )
    out = pl.pallas_call(
        flush,
        out_shape=jax.ShapeDtypeStruct((comps * rows_x, lanes), bf16),
        in_specs=[vmem],
        out_specs=any_space,
        scratch_shapes=[pltpu.SemaphoreType.DMA],
        compiler_params=pltpu.CompilerParams(vmem_limit_bytes=8 * 1024 * 1024),
    )(out)
    return out.reshape(comps, rows_x, lanes)


def solution(mesh):
    placed = (P(None, ("member", "pts"), "sub"), P(), P(), P("pts", "sub"))
    return jax.shard_map(
        functools.partial(shards, (mesh.shape["pts"], mesh.shape["sub"])),
        mesh=mesh,
        in_specs=placed,
        out_specs=P(None, ("member", "pts"), "sub"),
        check_vma=False,
    )
```

time: 35.2 us -> 32.1 us (0.912)
  Pallas kernels: 30.8 us -> 28.8 us
  local copies, waits for them, and re-layouts: 4.06 us -> 2.79 us
    pallas_call x1, Pallas kernels: 30.8 us -> 27.6 us  [shards(): pl.pallas_call(functools.partial(kernel, rows_x, chunks, plus_runs, minus...]
    unnamed x1 -> x2, local copies, waits for them, and re-layouts: 2.76 us -> 1.5 us
    pallas_call x0 -> x1, Pallas kernels: none -> 1.24 us  [shards(): pl.pallas_call(flush, out_shape=jax.ShapeDtypeStruct((comps * rows_x, lan...]
where the time goes in v2:
time: 32.1 us; the launch traced here: 31.6 us
  Pallas kernels  28.8 us (90%)
  local copies, waits for them, and re-layouts  2.79 us (9%)
    pallas_call x1, Pallas kernels, shards(): pl.pallas_call(functools.partial(kernel, rows_x, chunks, plus_runs, minus...  27.6 us
    unnamed x2, local copies, waits for them, and re-layouts  1.5 us
    reshape x1, local copies, waits for them, and re-layouts, shards(): speeds.reshape(1, comps)  1.3 us
    pallas_call x1, Pallas kernels, shards(): pl.pallas_call(flush, out_shape=jax.ShapeDtypeStruct((comps * rows_x, lan...  1.24 us

profile of v2, /device:TPU:1, one launch (start us, length us, event | category | flops | bytes accessed | tf_op | source)
XLA Modules:
  0.0 31.6 jit_solution(15805673875410902577)
XLA Ops:
  0.0 1.3 %reshape.10.speeds_ref = f32[1,1800]{1,0:T(1,128)} reshape(f32[1800]{0:T(1024)} %param.7) | data formatting | bytes 14400 | tf_op jit(solution)/shard_map/reshape | solution.py:361
  1.3 27.6 %shard_map.55.held = bf16[7200,128]{1,0:T(8,128)(2,1)} custom-call(bf16[7200,128]{1,0:T(8,128)(2,1)} %bitcast.2, bf16[1800,1800]{1,0:T(8,128)(2,1)} %inter_hbm.1, f32[1,1800]{1,0:T(1,128)} %reshape.10.speeds_ref, s32[4,128]{1,0:T(4,128)} %mask_ref.1, f32[4,72,128]{2,1,0:T(8,128)} %constant.2.clone.tabs_ref), custom_call_target="tpu_custom_call" | custom-call | tf_op jit(solution)/shard_map/pallas_call | solution.py:331
  28.9 0.0 copy-start
  28.9 1.5 %copy-done = bf16[7200,128]{1,0:T(8,128)(2,1)S(1)} copy-done((bf16[7200,128]{1,0:T(8,128)(2,1)S(1)}, bf16[7200,128]{1,0:T(8,128)(2,1)}, u32[]{:S(2)}) %copy-start) | copy-done | bytes 1843224
  30.4 1.2 %shard_map.56 = bf16[7200,128]{1,0:T(8,128)(2,1)} custom-call(bf16[7200,128]{1,0:T(8,128)(2,1)S(1)} %copy-done), custom_call_target="tpu_custom_call" | custom-call | tf_op jit(solution)/shard_map/pallas_call | solution.py:364
Async XLA Ops:
  28.9 1.5 %copy-start = (bf16[7200,128]{1,0:T(8,128)(2,1)S(1)}, bf16[7200,128]{1,0:T(8,128)(2,1)}, u32[]{:S(2)}) copy-start(bf16[7200,128]{1,0:T(8,128)(2,1)} %shard_map.55.held) | copy-start | bytes 5529604
